TPU v7x, 256 devices: a whole 4x4x8 slice. The times are simulated.
256 devices in a mesh: rows: 64 (over z, y, core), panel: 4 (over x).
Axes of the slice: x: 4, y: 4, z: 8, core: 2. Of those that a mesh axis runs over, the one named last changes fastest.
Arguments:
- pair_block: bfloat16 [2048, 16384], P('rows', 'panel'), may hold values from -6 to 6
- resolvent: float32 [16384, 16384], P('panel', 'rows'), may hold values from -0.046875 to 0.046875
- virt_coef: bfloat16 [1024, 11200], P('rows', 'panel'), may hold values from -0.1875 to 0.1875
- slot_row: int32 [2048], replicated, may hold values from 0 to 2047, each once
Outputs:
- backward: float32 [2, 11200, 16384], P(None, 'panel', 'rows')
Inputs may be any that keep to these rules, and one draw needn't show every extreme that they name: `slot_row`: every pair row appears exactly once.
All inputs are finite; a program needn't handle non-finite values.
Results may differ from a plain program's by a relative error of at most 0.0041.
Values may be sent and summed in bfloat16 or wider, within the bound.
A program may use at most 128 MiB of HBM per device.

v0:
```python
import jax
import jax.numpy as jnp
from jax import lax
from jax.sharding import PartitionSpec as P

OCC_B = 2


def body(pair_block, resolvent, virt_coef, slot_row):
    resolvent_round = resolvent.astype(jnp.bfloat16)
    gathered = None
    partial_sum = jnp.dot(
        lax.all_gather(pair_block, "rows", axis=0, tiled=True),
        resolvent_round,
        preferred_element_type=jnp.float32,
    )
    gathered = lax.psum(partial_sum, "panel").astype(jnp.bfloat16)
    grouped = jnp.take(gathered, slot_row, axis=0)
    grouped = grouped.reshape(OCC_B, slot_row.shape[0] // OCC_B, gathered.shape[1])
    coef_all = lax.all_gather(virt_coef, "rows", axis=0, tiled=True)
    return jnp.einsum("am,oac->omc", coef_all, grouped, preferred_element_type=jnp.float32)


def solution(mesh):
    placed = (P("rows", "panel"), P("panel", "rows"), P("rows", "panel"), P())
    return jax.shard_map(
        body, mesh=mesh, in_specs=placed, out_specs=P(None, "panel", "rows"), check_vma=False
    )
```

profile of v0, /device:TPU:1, one launch (start us, length us, event | category | flops | bytes accessed | tf_op | source)
XLA Modules:
  0.0 209.5 jit_solution(6740521300446435897)
XLA Ops:
  6.5 0.0 all-gather.3.cloned.1.call-start
  6.5 0.7 all-gather.3.cloned.1.call-update
  7.3 0.0 all-gather.5.cloned.1.call-start
  7.3 0.7 all-gather.5.cloned.1.call-update
  8.0 0.7 compare_and_fusion
  8.7 0.7 fusion.10
  9.4 104.2 %all-gather.3.cloned.1.call-done = bf16[2048,4096]{1,0:T(8,128)(2,1)} async-done(((bf16[32,4096]{1,0:T(8,128)(2,1)}), bf16[2048,4096]{1,0:T(8,128)(2,1)}) %all-gather.3.cloned.1.call-update) | async-done | bytes 16777232 | tf_op jit(solution)/shard_map/all_gather | solution.py:13
  113.6 9.3 %fusion.5 = f32[2048,256]{1,0:T(8,128)S(1)} fusion(bf16[2048,4096]{1,0:T(8,128)(2,1)} %all-gather.3.cloned.1.call-done, f32[4096,256]{1,0:T(8,128)} %param.5), kind=kOutput, calls=%fused_computation.4 | convolution fusion | flops 4296015872 | bytes 23068672 | tf_op jit(solution)/shard_map/dot_general | solution.py:12
  122.9 42.3 %all-reduce.1 = bf16[2048,256]{1,0:T(8,128)(2,1)S(1)} all-reduce(f32[2048,256]{1,0:T(8,128)S(1)} %fusion.5), channel_id=1, replica_groups=mesh['rows'=64,'panel'=4] {'panel'}, use_global_device_ids=true, to_apply=%region_0.0 | all-reduce | flops 524288 | bytes 3145728 | tf_op jit(solution)/shard_map/psum | solution.py:17
  165.2 7.5 %gather_fusion = bf16[2048,256]{1,0:T(8,128)(2,1)S(1)} fusion(bf16[2048,256]{1,0:T(8,128)(2,1)S(1)} %all-reduce.1, s32[2048]{0:T(1024)S(1)} %fusion.10), kind=kCustom, calls=%fused_computation | custom fusion | bytes 2105344 | tf_op jit(solution)/shard_map/jit(_take)/gather | solution.py:18
  172.7 20.7 %all-gather.5.cloned.1.call-done = bf16[1024,2800]{1,0:T(8,128)(2,1)} async-done(((bf16[16,2800]{1,0:T(8,128)(2,1)}), bf16[1024,2800]{1,0:T(8,128)(2,1)}) %all-gather.5.cloned.1.call-update) | async-done | bytes 5734416 | tf_op jit(solution)/shard_map/all_gather | solution.py:20
  193.4 9.2 %fusion.2 = f32[2,2800,256]{2,1,0:T(8,128)} fusion(bf16[1024,2800]{1,0:T(8,128)(2,1)} %all-gather.5.cloned.1.call-done, bf16[2,1024,256]{2,1,0:T(8,128)(2,1)S(1)} %bitcast.9, pred[2,1024]{1,0:T(4,128)(4,1)S(1)} %broadcast_in_dim.14), kind=kOutput, calls=%fused_computation.3 | convolution fusion | flops 2936537088 | bytes 12519424 | tf_op jit(solution)/shard_map/am,oac->omc/dot_general | solution.py:21
  (1 shorter events, 0.0 us)
Async XLA Ops:
  6.5 107.1 %all-gather.3.cloned.1.call-start = ((), (), s32[]{:S(2)}) async-start(), calls=%async_computation | async-start | bytes 17039360 | tf_op jit(solution)/shard_map/all_gather | solution.py:13
  7.3 186.2 %all-gather.5.cloned.1.call-start = ((), (), s32[]{:S(2)}) async-start(), calls=%async_computation.1 | async-start | bytes 5857280 | tf_op jit(solution)/shard_map/all_gather | solution.py:20
Sparse Core Ops, SparseCore 0:
  10.1 103.4 all-gather.2
  116.3 77.0 all-gather.4
where the time goes:
time: 210 us; the launch traced here: 209 us
  waiting for transfers between devices  126 us (60%)
  blocking collectives  42.3 us (20%)
  matrix products  18.5 us (9%)
  between operations  13.4 us (6%)
  local copies, waits for them, and re-layouts  7.51 us (4%)
    all_gather x1, waiting for transfers between devices, body(): lax.all_gather(pair_block, 'rows', axis=0, tiled=True)  104 us
    psum x1, blocking collectives, body(): gathered = lax.psum(partial_sum, 'panel').astype(jnp.bfloat16)  42.3 us
    all_gather x1, waiting for transfers between devices, body(): coef_all = lax.all_gather(virt_coef, 'rows', axis=0, tiled=True)  20.7 us
    dot_general x1, matrix products, body(): jnp.dot(lax.all_gather(pair_block, 'rows', axis=0, tiled=True), resolvent...  9.32 us
    dot_general x1, matrix products, body(): jnp.einsum('am,oac->omc', coef_all, grouped, preferred_element_type=jnp.f...  9.22 us
    gather x1, local copies, waits for them, and re-layouts, body(): grouped = jnp.take(gathered, slot_row, axis=0)  7.5 us
  transfers between devices with their start and end apart: 2, of which 2 were waited for; matrix products, arithmetic and copies ran while one was open for 9% of the time, Pallas kernels for 0%

commit v1 on v0

v1 whole, which is shorter than its diff:
```python
import functools

import jax
import jax.numpy as jnp
from jax import lax
from jax.experimental import pallas as pl
from jax.experimental.pallas import tpu as pltpu
from jax.sharding import PartitionSpec as P

MESH = pl.DeviceIdType.MESH

NX, NY, NZ, NC = 4, 4, 8, 2
ROWS, KB, PB = 32, 4096, 256
CR, CM, CP = 16, 2800, 2816
KA, CA = 1664, 1152

ORDER = (
    (0, 1, 0), (0, 3, 0), (1, 0, 1), (1, 0, 7), (1, 1, 0), (1, 3, 0), (0, 0, 1), (0, 0, 7), (0, 2, 0), (0, 1, 1),
    (0, 1, 7), (1, 3, 1), (0, 3, 1), (0, 3, 7), (1, 1, 1), (1, 3, 7), (1, 1, 7), (1, 0, 2), (1, 0, 6), (1, 2, 0),
    (5, 0, 0), (0, 0, 2), (0, 0, 6), (1, 2, 1), (0, 2, 1), (0, 2, 7), (5, 1, 0), (1, 3, 2), (0, 1, 2), (0, 1, 6),
    (6, 0, 0), (1, 2, 7), (5, 7, 0), (1, 3, 6), (0, 3, 2), (0, 3, 6), (1, 1, 2), (6, 1, 0), (1, 1, 6), (1, 0, 3),
    (1, 0, 5), (7, 0, 0), (1, 2, 2), (6, 7, 0), (0, 0, 3), (0, 0, 5), (1, 2, 6), (0, 2, 2), (0, 2, 6), (5, 2, 0),
    (5, 6, 0), (1, 3, 3), (7, 1, 0), (7, 7, 0), (0, 1, 3), (0, 1, 5), (1, 1, 3), (1, 3, 5), (0, 3, 3), (0, 3, 5),
    (1, 1, 5), (6, 2, 0), (6, 6, 0), (1, 2, 3), (0, 2, 5), (4, 0, 0), (1, 0, 4), (0, 0, 4), (1, 2, 5), (5, 5, 0),
    (3, 1, 0), (3, 3, 0), (3, 0, 7), (0, 2, 3), (5, 3, 0), (2, 1, 0), (2, 3, 0), (2, 0, 7), (7, 2, 0), (7, 6, 0),
    (0, 1, 4), (3, 0, 6), (0, 3, 4), (2, 1, 7), (1, 1, 4), (1, 3, 4), (6, 5, 0), (2, 3, 7), (3, 0, 1), (3, 2, 0),
    (3, 3, 7), (2, 0, 6), (2, 0, 1), (3, 1, 7), (3, 3, 6), (6, 3, 0), (3, 0, 5), (2, 2, 0), (2, 1, 6), (3, 1, 6),
    (0, 2, 4), (3, 3, 1), (2, 3, 6), (2, 1, 1), (2, 0, 5), (8, 0, 0), (2, 3, 1), (3, 3, 5), (2, 2, 7), (1, 2, 4),
    (5, 4, 0), (2, 1, 5), (3, 1, 1), (3, 0, 2), (3, 2, 7), (2, 3, 5), (2, 0, 2), (7, 3, 0), (7, 5, 0), (3, 1, 5),
    (2, 2, 1), (3, 2, 6), (2, 2, 6), (2, 1, 2), (2, 3, 2), (3, 0, 3), (3, 2, 1), (3, 3, 2), (2, 0, 3), (2, 2, 2),
    (3, 1, 2), (3, 2, 5), (2, 2, 5), (2, 1, 3), (2, 3, 3), (6, 4, 0), (3, 0, 4), (8, 1, 0), (8, 7, 0), (2, 0, 4),
    (3, 1, 3), (3, 3, 3), (2, 2, 3), (3, 2, 2), (2, 1, 4), (2, 3, 4), (3, 1, 4), (3, 3, 4), (2, 2, 4), (8, 2, 0),
    (8, 6, 0), (3, 2, 3), (7, 4, 0), (3, 2, 4), (8, 3, 0), (8, 5, 0), (8, 4, 0),
)


def kernel(pair, res, coef, slots, ct, grouped, blocks, weights, stage, coefs, wide, parts, other, final, gamma, total,
           column, res_sem, block_sem, coef_sem, send_sem, half_sem, plane_sem):
    row, x = lax.axis_index("rows"), lax.axis_index("panel")
    core, y, z = row % NC, (row // NC) % NY, row // (NC * NY)
    turn = 1 - 2 * core
    mate = row + turn
    bf16, f32 = jnp.bfloat16, jnp.float32

    def at(dy, dz):
        return (y + NY - turn * dy) % NY, (z + NZ - turn * dz) % NZ

    def device(dy, dz):
        ty, tz = (y + NY + turn * dy) % NY, (z + NZ + turn * dz) % NZ
        return ((tz * NY + ty) * NC + core, x)

    def remote(src, dst, sent, got, to):
        return pltpu.make_async_remote_copy(
            src_ref=src, dst_ref=dst, send_sem=sent, recv_sem=got, device_id=to, device_id_type=MESH
        )

    step = KB // 4
    loads = [
        pltpu.make_async_copy(res.at[pl.ds(i * step, step)], stage.at[pl.ds(i * step, step)], res_sem.at[i])
        for i in range(4)
    ]
    for load in loads:
        load.start()

    barrier = pltpu.get_barrier_semaphore()
    peers = [device(1, 0), device(-1, 0), device(0, 1), device(0, -1), (mate, x)]
    peers += [(r, (x + d) % NX) for d in range(1, NX) for r in (row, mate)]
    for peer in peers:
        pl.semaphore_signal(barrier, inc=1, device_id=peer, device_id_type=MESH)
    pl.semaphore_wait(barrier, len(peers))

    def piece(kind, place):
        chip, plane = place[1] * NY + place[0], None
        if kind < 2:
            return blocks.at[chip, :, pl.ds(0, KA) if kind == 0 else pl.ds(KA, KB - KA)]
        return coefs.at[chip * NC + core, :, pl.ds(0, CA) if kind == 2 else pl.ds(CA, CP - CA)]

    def arrival(kind, place):
        sems = block_sem if kind < 2 else coef_sem
        return sems.at[kind % 2, place[1] * NY + place[0]]

    def pass_on(kind, dy, dz):
        place = at(dy, dz)
        ref = piece(kind, place)
        src = ref
        if kind < 2 and dy == 0 and dz == 0:
            src = pair.at[:, pl.ds(0, KA) if kind == 0 else pl.ds(KA, KB - KA)]
        along_y = []
        along_z = []
        if kind % 2 == 0:
            if dz == 0:
                along_y = [1] * (dy in (0, 1)) + [-1] * (dy == 0)
                along_z = [1, -1]
            else:
                along_z = [1] * (dz in (1, 2, 3)) + [-1] * (dz in (6, 7))
        else:
            if dy == 0:
                along_z = [1] * (dz in (0, 1, 2, 3)) + [-1] * (dz in (0, 6, 7))
                along_y = [1, -1]
            elif dy == 1:
                along_y = [1]
        hops = [(d, 0) for d in along_y] + [(0, d) for d in along_z]
        for hop in hops:
            remote(src, ref, send_sem.at[kind], arrival(kind, place), device(*hop)).start()

    pass_on(0, 0, 0)
    pass_on(1, 0, 0)

    chip = z * NY + y
    blocks[chip] = pair[...]
    own = coef[...]
    coefs[row] = jnp.concatenate([own, jnp.zeros((CR, CP - CM), bf16)], axis=1)
    for i in range(16):
        wide_row = jnp.broadcast_to(slots[i : i + 1, :].astype(f32), (128, 128))
        column[pl.ds(i * 128, 128), :] = jnp.transpose(wide_row).astype(jnp.int32)
    total[...] = jnp.zeros_like(total)
    for i in range(5):
        if i < 4:
            loads[i].wait()
            weights[core, pl.ds(i * step, step), :] = stage[pl.ds(i * step, step), :].astype(bf16)
        if i > 0:
            ref = weights.at[core, pl.ds((i - 1) * step, step)]
            remote(ref, ref, half_sem.at[0], half_sem.at[1], (mate, x)).start()
    whole = weights.at[1 - core]
    remote(whole, whole, half_sem.at[0], half_sem.at[1], (mate, x)).wait_recv()

    def share_coefs(place):
        ref = coefs.at[(place[1] * NY + place[0]) * NC + core]
        remote(ref, ref, send_sem.at[4], plane_sem.at[2, place[1]], (mate, x)).start()

    def multiply(dz):
        _, plane = at(0, dz)
        first = plane * NY
        for half in range(NC):
            def over(k, carry):
                cols = pl.ds(pl.multiple_of(k * 1024, 1024), 1024)
                left = blocks[pl.ds(first, NY), :, cols].reshape(NY * ROWS, 1024)
                prod = jnp.dot(left, weights[half, cols, :], preferred_element_type=f32)
                return carry + prod
            prod = lax.fori_loop(0, 4, over, jnp.zeros((NY * ROWS, PB), f32)).reshape(NY, ROWS, PB)
            wide[plane, :, half] = prod
            parts[plane, :, half] = prod.astype(bf16)
        for d in range(1, NX):
            to = (x + d) % NX
            remote(parts.at[plane, to], other.at[plane, d - 1], send_sem.at[5], plane_sem.at[0, plane], (row, to)).start()

    def add_up(dz):
        _, plane = at(0, dz)
        ref = other.at[plane]
        remote(ref, ref, send_sem.at[5], plane_sem.at[0, plane], (row, x)).wait_recv()
        value = wide[plane, x]
        for d in range(NX - 1):
            value = value + other[plane, d].astype(f32)
        value = value.astype(bf16)
        final[plane] = value
        spot = plane * (NY * NC) + x * NC + core
        gamma[spot] = final[plane, core]
        remote(final.at[plane, 1 - core], gamma.at[spot], send_sem.at[6], plane_sem.at[1, plane], (mate, x)).start()
        for d in range(1, NX):
            for c in range(NC):
                to = ((z * NY + y) * NC + c, (x + d) % NX)
                remote(final.at[plane, c], gamma.at[spot], send_sem.at[6], plane_sem.at[1, plane], to).start()

    def select(dz):
        _, plane = at(0, dz)
        ref = gamma.at[pl.ds(0, NY * NC - 1)]
        remote(ref, ref, send_sem.at[6], plane_sem.at[1, plane], (mate, x)).wait_recv()
        rows = gamma[pl.ds(plane * (NY * NC), NY * NC)].reshape(NY * NC * ROWS, PB)
        base = plane * (NY * NC * ROWS)
        lanes = lax.broadcasted_iota(jnp.int32, (256, 128), 1)

        def over(i, carry):
            at_rows = pl.ds(pl.multiple_of(i * 256, 256), 256)
            ids = column[at_rows, :] - base
            pick = jnp.concatenate(
                [jnp.where(ids == lanes + h * 128, 1.0, 0.0).astype(bf16) for h in range(2)], axis=1
            )
            total[at_rows, :] += jnp.dot(pick, rows, preferred_element_type=f32)
            return carry

        lax.fori_loop(0, 8, over, 0)

    def transpose(dz):
        _, plane = at(0, dz)
        ref = coefs.at[pl.ds(0, NY)]
        remote(ref, ref, send_sem.at[4], plane_sem.at[2, plane], (mate, x)).wait_recv()
        out_cols = pl.ds(pl.multiple_of(plane * 128, 128), 128)

        def over(i, carry):
            cols = pl.ds(pl.multiple_of(i * 1408, 128), 1408)
            tile = coefs[pl.ds(plane * (NY * NC), NY * NC), :, cols].reshape(128, 1408)
            ct[cols, out_cols] = jnp.transpose(tile)
            return carry

        lax.fori_loop(0, 2, over, 0)

    seen = {}
    for kind, dy, dz in ORDER:
        if kind < 4:
            place = at(dy, dz)
            ref = piece(kind, place)
            remote(ref, ref, send_sem.at[kind], arrival(kind, place), (mate, x)).wait_recv()
            pass_on(kind, dy, dz)
            if kind >= 2:
                seen[dy, dz] = seen.get((dy, dz), 0) + 1
                if seen[dy, dz] == 2:
                    share_coefs(place)
        elif kind == 4:
            pass_on(3, 0, 0)
            pass_on(2, 0, 0)
            share_coefs(at(0, 0))
        else:
            {5: multiply, 6: add_up, 7: select, 8: transpose}[kind](dy)

    grouped[...] = total[...].astype(bf16)

    def drained(ref, sem):
        remote(ref, ref, sem, half_sem.at[1], (mate, x)).wait_send()

    sends = NY * NZ - 1
    drained(blocks.at[pl.ds(0, sends), :, pl.ds(0, KA)], send_sem.at[0])
    drained(blocks.at[pl.ds(0, sends), :, pl.ds(KA, KB - KA)], send_sem.at[1])
    drained(coefs.at[pl.ds(0, sends), :, pl.ds(0, CA)], send_sem.at[2])
    drained(coefs.at[pl.ds(0, sends), :, pl.ds(CA, CP - CA)], send_sem.at[3])
    drained(coefs.at[pl.ds(0, NY * NZ)], send_sem.at[4])
    drained(other, send_sem.at[5])
    drained(gamma.at[pl.ds(0, NZ * (NY * NC - 1))], send_sem.at[6])
    drained(whole, half_sem.at[0])


def finish(ct, grouped, out):
    out[0] = jnp.dot(ct[...], grouped[...], preferred_element_type=jnp.float32)


def body(pair_block, resolvent, virt_coef, slot_row):
    vmem = pl.BlockSpec(memory_space=pltpu.VMEM)
    dma = pltpu.SemaphoreType.DMA
    bf16, f32 = jnp.bfloat16, jnp.float32
    ct, grouped = pl.pallas_call(
        kernel,
        out_shape=(
            jax.ShapeDtypeStruct((CP, NZ * NY * NC * CR), bf16),
            jax.ShapeDtypeStruct((NZ * NY * NC * ROWS, PB), bf16),
        ),
        in_specs=[vmem, pl.BlockSpec(memory_space=pl.ANY), vmem, vmem],
        out_specs=(vmem, vmem),
        scratch_shapes=[
            pltpu.VMEM((NY * NZ, ROWS, KB), bf16),
            pltpu.VMEM((NC, KB, PB), bf16),
            pltpu.VMEM((KB, PB), f32),
            pltpu.VMEM((NY * NZ * NC, CR, CP), bf16),
            pltpu.VMEM((NZ, NY, NC, ROWS, PB), f32),
            pltpu.VMEM((NZ, NY, NC, ROWS, PB), bf16),
            pltpu.VMEM((NZ, NX - 1, NC, ROWS, PB), bf16),
            pltpu.VMEM((NZ, NC, ROWS, PB), bf16),
            pltpu.VMEM((NZ * NY * NC, ROWS, PB), bf16),
            pltpu.VMEM((NZ * NY * NC * ROWS, PB), f32),
            pltpu.VMEM((NZ * NY * NC * ROWS, 128), jnp.int32),
            dma((4,)),
            dma((2, NY * NZ)),
            dma((2, NY * NZ)),
            dma((7,)),
            dma((2,)),
            dma((3, NZ)),
        ],
        compiler_params=pltpu.CompilerParams(
            collective_id=0, has_side_effects=True, vmem_limit_bytes=46 * 1024 * 1024
        ),
    )(pair_block, resolvent, virt_coef, slot_row.reshape(16, 128))
    width = NZ * NY * NC * CR
    tall = 400
    return pl.pallas_call(
        finish,
        grid=(CM // tall, 2),
        out_shape=jax.ShapeDtypeStruct((2, CM, PB), f32),
        in_specs=[
            pl.BlockSpec((tall, width), lambda i, o: (i, 0)),
            pl.BlockSpec((width, PB), lambda i, o: (o, 0)),
        ],
        out_specs=pl.BlockSpec((1, tall, PB), lambda i, o: (o, i, 0)),
        compiler_params=pltpu.CompilerParams(vmem_limit_bytes=16 * 1024 * 1024),
        cost_estimate=pl.CostEstimate(flops=4 * CM * width * PB, bytes_accessed=12000000, transcendentals=0),
    )(ct, grouped)


def solution(mesh):
    placed = (P("rows", "panel"), P("panel", "rows"), P("rows", "panel"), P())
    return jax.shard_map(
        body, mesh=mesh, in_specs=placed, out_specs=P(None, "panel", "rows"), check_vma=False
    )
```

time: 210 us -> 114 us (0.54)
  waiting for transfers between devices: 126 us -> 0 us
  Pallas kernels: 0 us -> 106 us
  blocking collectives: 42.3 us -> 0 us
  matrix products: 18.5 us -> 0 us
  between operations: 13.4 us -> 0.02 us
    all_gather x2 -> x0, waiting for transfers between devices: 125 us -> none  [the longest x1 104 us: body(): lax.all_gather(pair_block, 'rows', axis=0, tiled=True)]
    pallas_call x0 -> x2, Pallas kernels: none -> 106 us  [the longest x1 97.7 us: body(): pl.pallas_call(kernel, out_shape=(jax.ShapeDtypeStruct((CP, NZ * NY * NC...]
    psum x1 -> x0, blocking collectives: 42.3 us -> none  [body(): gathered = lax.psum(partial_sum, 'panel').astype(jnp.bfloat16)]
    dot_general x2 -> x0, matrix products: 18.5 us -> none  [the longest x1 9.32 us: body(): jnp.dot(lax.all_gather(pair_block, 'rows', axis=0, tiled=True), resolvent...]
    gather x1 -> x0, local copies, waits for them, and re-layouts: 7.5 us -> none  [body(): grouped = jnp.take(gathered, slot_row, axis=0)]
    unnamed x0 -> x10, local copies, waits for them, and re-layouts: none -> 7.35 us
  transfers between devices with their start and end apart: 2 -> 0, of which waited for: 2 -> 0; matrix products, arithmetic and copies ran while one was open for 9% -> 0% of each run, Pallas kernels for 0% -> 0%
where the time goes in v1:
time: 114 us; the launch traced here: 113 us
  Pallas kernels  106 us (93%)
  local copies, waits for them, and re-layouts  7.35 us (6%)
    pallas_call x1, Pallas kernels, body(): pl.pallas_call(kernel, out_shape=(jax.ShapeDtypeStruct((CP, NZ * NY * NC...  97.7 us
    pallas_call x1, Pallas kernels, body(): pl.pallas_call(finish, grid=(CM // tall, 2), out_shape=jax.ShapeDtypeStru...  8.3 us
    unnamed x10, local copies, waits for them, and re-layouts  7.35 us

profile of v1, /device:TPU:1, one launch (start us, length us, event | category | flops | bytes accessed | tf_op | source)
XLA Modules:
  0.0 113.3 jit_solution(3526768406402394814)
XLA Ops:
  0.0 0.0 copy-start.1
  0.0 2.2 %copy-done.1 = f32[4096,256]{1,0:T(8,128)S(1)} copy-done((f32[4096,256]{1,0:T(8,128)S(1)}, f32[4096,256]{1,0:T(8,128)}, u32[]{:S(2)}) %copy-start.1) | copy-done | bytes 4194328
  2.2 0.0 copy-start.2
  2.2 0.9 copy-done.2
  3.1 0.0 copy-start.3
  3.1 0.9 copy-done.3
  4.0 0.0 copy-start.4
  4.0 0.7 copy-done.4
  4.7 97.7 %shard_map.46 = (bf16[2816,1024]{1,0:T(8,128)(2,1)}, bf16[2048,256]{1,0:T(8,128)(2,1)S(1)}) custom-call(bf16[32,4096]{1,0:T(8,128)(2,1)S(1)} %copy-done.2, f32[4096,256]{1,0:T(8,128)S(1)} %copy-done.1, bf16[16,2800]{1,0:T(8,128)(2,1)S(1)} %copy-done.3, s32[16,128]{1,0:T(8,128)S(1)} %bitcast.1), custom_call_target="tpu_custom_call" | custom-call | tf_op jit(solution)/shard_map/pallas_call | solution.py:239
  102.4 0.0 copy-start
  102.4 2.6 %copy-done = bf16[2816,1024]{1,0:T(8,128)(2,1)S(1)} copy-done((bf16[2816,1024]{1,0:T(8,128)(2,1)S(1)}, bf16[2816,1024]{1,0:T(8,128)(2,1)}, u32[]{:S(2)}) %copy-start) | copy-done | bytes 5767192
  105.0 8.3 %shard_map.47 = f32[2,2800,256]{2,1,0:T(8,128)} custom-call(bf16[2816,1024]{1,0:T(8,128)(2,1)S(1)} %copy-done, bf16[2048,256]{1,0:T(8,128)(2,1)S(1)} %get-tuple-element.8.grouped), custom_call_target="tpu_custom_call" | custom-call | flops 2936012800 | bytes 12000000 | tf_op jit(solution)/shard_map/pallas_call | solution.py:272
Async XLA Ops:
  0.0 2.2 %copy-start.1 = (f32[4096,256]{1,0:T(8,128)S(1)}, f32[4096,256]{1,0:T(8,128)}, u32[]{:S(2)}) copy-start(f32[4096,256]{1,0:T(8,128)} %res.1) | copy-start | bytes 12582916
  2.2 0.9 copy-start.2
  3.1 0.9 copy-start.3
  4.0 0.7 copy-start.4
  102.4 2.6 %copy-start = (bf16[2816,1024]{1,0:T(8,128)(2,1)S(1)}, bf16[2816,1024]{1,0:T(8,128)(2,1)}, u32[]{:S(2)}) copy-start(bf16[2816,1024]{1,0:T(8,128)(2,1)} %get-tuple-element.7.ct) | copy-start | bytes 17301508

commit v2 on v1

v2 whole, which is shorter than its diff:
```python
import functools

import jax
import jax.numpy as jnp
from jax import lax
from jax.experimental import pallas as pl
from jax.experimental.pallas import tpu as pltpu
from jax.sharding import PartitionSpec as P

MESH = pl.DeviceIdType.MESH

NX, NY, NZ, NC = 4, 4, 8, 2
ROWS, KB, PB = 32, 4096, 256
CHUNKS = 7
CR, CM, CP = 16, 2800, 2816
KA, CA = 1664, 1152

ORDER = (
    (9, 0, 0), (9, 1, 0), (9, 2, 0), (9, 3, 0), (9, 4, 0), (9, 5, 0), (0, 1, 0), (0, 3, 0), (0, 0, 1), (0, 0, 7),
    (1, 1, 0), (1, 3, 0), (1, 0, 1), (1, 0, 7), (0, 2, 0), (0, 1, 1), (0, 1, 7), (0, 3, 1), (0, 3, 7), (1, 2, 0),
    (5, 0, 0), (1, 3, 1), (5, 0, 1), (0, 0, 2), (0, 0, 6), (1, 1, 1), (1, 3, 7), (6, 0, 0), (1, 1, 7), (1, 0, 2),
    (1, 0, 6), (1, 2, 1), (0, 2, 1), (0, 2, 7), (5, 1, 0), (5, 1, 1), (7, 0, 0), (7, 0, 1), (0, 1, 2), (0, 1, 6),
    (1, 2, 7), (5, 7, 0), (1, 3, 2), (5, 7, 1), (6, 1, 0), (0, 3, 2), (0, 3, 6), (1, 1, 2), (1, 3, 6), (0, 0, 3),
    (0, 0, 5), (6, 7, 0), (1, 1, 6), (1, 2, 2), (1, 0, 3), (1, 0, 5), (7, 1, 0), (1, 2, 6), (7, 1, 1), (7, 7, 0),
    (7, 7, 1), (0, 2, 2), (0, 2, 6), (5, 2, 0), (5, 2, 1), (5, 6, 0), (5, 6, 1), (0, 1, 3), (0, 1, 5), (1, 1, 3),
    (1, 3, 3), (6, 2, 0), (0, 3, 3), (0, 3, 5), (6, 6, 0), (1, 1, 5), (1, 3, 5), (4, 0, 0), (0, 0, 4), (0, 2, 5),
    (1, 2, 3), (1, 0, 4), (7, 2, 0), (3, 3, 0), (3, 0, 7), (7, 2, 1), (7, 6, 0), (2, 3, 0), (2, 0, 7), (1, 2, 5),
    (0, 2, 3), (5, 3, 0), (5, 3, 1), (3, 1, 0), (5, 5, 0), (0, 1, 4), (5, 5, 1), (2, 1, 0), (3, 0, 6), (7, 6, 1),
    (2, 3, 7), (1, 3, 4), (2, 0, 6), (0, 3, 4), (6, 3, 0), (3, 3, 7), (3, 0, 1), (2, 1, 7), (1, 1, 4), (6, 5, 0),
    (2, 0, 1), (3, 3, 6), (3, 1, 7), (3, 0, 5), (2, 3, 1), (3, 2, 0), (2, 3, 6), (2, 2, 0), (3, 3, 1), (2, 0, 5),
    (3, 1, 6), (0, 2, 4), (2, 1, 6), (3, 3, 5), (8, 0, 0), (3, 1, 1), (2, 1, 1), (2, 3, 5), (8, 0, 1), (7, 3, 0),
    (7, 3, 1), (2, 2, 7), (3, 0, 2), (7, 5, 0), (1, 2, 4), (5, 4, 0), (2, 1, 5), (2, 0, 2), (3, 2, 7), (2, 3, 2),
    (3, 1, 5), (2, 2, 1), (5, 4, 1), (2, 1, 2), (3, 2, 6), (7, 5, 1), (2, 2, 6), (3, 0, 3), (3, 3, 2), (3, 2, 1),
    (2, 0, 3), (3, 1, 2), (2, 3, 3), (2, 2, 2), (3, 2, 5), (8, 1, 0), (2, 1, 3), (8, 1, 1), (2, 2, 5), (6, 4, 0),
    (3, 0, 4), (3, 1, 3), (3, 3, 3), (2, 0, 4), (8, 7, 0), (3, 2, 2), (2, 3, 4), (8, 7, 1), (2, 2, 3), (2, 1, 4),
    (8, 2, 0), (8, 2, 1), (8, 6, 0), (3, 1, 4), (3, 3, 4), (8, 6, 1), (2, 2, 4), (3, 2, 3), (7, 4, 0), (7, 4, 1),
    (10, 0, 0), (8, 3, 0), (3, 2, 4), (8, 3, 1), (8, 5, 0), (8, 5, 1), (8, 4, 0), (8, 4, 1),
)


def kernel(pair, res, coef, slots, ct, grouped, blocks, weights, stage, coefs, wide, parts, other, final, gamma, total,
           column, own_coef, own_slots, turned, rounded, load_sem, out_sem, block_sem, coef_sem, send_sem, half_sem,
           plane_sem):
    row, x = lax.axis_index("rows"), lax.axis_index("panel")
    core, y, z = row % NC, (row // NC) % NY, row // (NC * NY)
    turn = 1 - 2 * core
    mate = row + turn
    bf16, f32 = jnp.bfloat16, jnp.float32

    def at(dy, dz):
        return (y + NY - turn * dy) % NY, (z + NZ - turn * dz) % NZ

    def device(dy, dz):
        ty, tz = (y + NY + turn * dy) % NY, (z + NZ + turn * dz) % NZ
        return ((tz * NY + ty) * NC + core, x)

    def remote(src, dst, sent, got, to):
        return pltpu.make_async_remote_copy(
            src_ref=src, dst_ref=dst, send_sem=sent, recv_sem=got, device_id=to, device_id_type=MESH
        )

    own = z * NY + y
    step = KB // 4
    load_pair = pltpu.make_async_copy(pair, blocks.at[own], load_sem.at[4])
    load_pair.start()
    loads = [
        pltpu.make_async_copy(res.at[pl.ds(i * step, step)], stage.at[pl.ds(i * step, step)], load_sem.at[i])
        for i in range(4)
    ]
    load_coef = pltpu.make_async_copy(coef, own_coef, load_sem.at[5])
    load_slots = pltpu.make_async_copy(slots, own_slots, load_sem.at[6])
    for load in loads + [load_coef, load_slots]:
        load.start()

    barrier = pltpu.get_barrier_semaphore()
    peers = [device(1, 0), device(-1, 0), device(0, 1), device(0, -1), (mate, x)]
    peers += [(r, (x + d) % NX) for d in range(1, NX) for r in (row, mate)]
    for peer in peers:
        pl.semaphore_signal(barrier, inc=1, device_id=peer, device_id_type=MESH)
    load_pair.wait()
    pl.semaphore_wait(barrier, len(peers))

    def piece(kind, place):
        chip = place[1] * NY + place[0]
        if kind < 2:
            return blocks.at[chip, :, pl.ds(0, KA) if kind == 0 else pl.ds(KA, KB - KA)]
        return coefs.at[chip * NC + core, :, pl.ds(0, CA) if kind == 2 else pl.ds(CA, CP - CA)]

    def arrival(kind, place):
        sems = block_sem if kind < 2 else coef_sem
        return sems.at[kind % 2, place[1] * NY + place[0]]

    def pass_on(kind, dy, dz):
        place = at(dy, dz)
        ref = piece(kind, place)
        along_y = []
        along_z = []
        if kind % 2 == 0:
            if dz == 0:
                along_y = [1] * (dy in (0, 1)) + [-1] * (dy == 0)
                along_z = [1, -1]
            else:
                along_z = [1] * (dz in (1, 2, 3)) + [-1] * (dz in (6, 7))
        else:
            if dy == 0:
                along_z = [1] * (dz in (0, 1, 2, 3)) + [-1] * (dz in (0, 6, 7))
                along_y = [1, -1]
            elif dy == 1:
                along_y = [1]
        for hop in [(d, 0) for d in along_y] + [(0, d) for d in along_z]:
            remote(ref, ref, send_sem.at[kind], arrival(kind, place), device(*hop)).start()

    def share_coefs(place):
        ref = coefs.at[(place[1] * NY + place[0]) * NC + core]
        remote(ref, ref, send_sem.at[4], plane_sem.at[2, place[1]], (mate, x)).start()

    whole = weights.at[1 - core]

    def prepare(i, _):
        if i < 4:
            loads[i].wait()
            weights[core, pl.ds(i * step, step), :] = stage[pl.ds(i * step, step), :].astype(bf16)
        if 0 < i < 5:
            ref = weights.at[core, pl.ds((i - 1) * step, step)]
            remote(ref, ref, half_sem.at[0], half_sem.at[1], (mate, x)).start()
        if i == 5:
            load_coef.wait()
            coefs[row] = jnp.concatenate([own_coef[...], jnp.zeros((CR, CP - CM), bf16)], axis=1)
            load_slots.wait()
            for j in range(16):
                wide_row = jnp.broadcast_to(own_slots[j : j + 1, :].astype(f32), (128, 128))
                column[pl.ds(j * 128, 128), :] = jnp.transpose(wide_row).astype(jnp.int32)

    multiplied = set()

    def multiply(dz, half):
        if not multiplied:
            remote(whole, whole, half_sem.at[0], half_sem.at[1], (mate, x)).wait_recv()
        multiplied.add((dz, half))
        _, plane = at(0, dz)
        left = blocks[pl.ds(plane * NY, NY)].reshape(NY * ROWS, KB)
        prod = jnp.dot(left, weights[half], preferred_element_type=f32).reshape(NY, ROWS, PB)
        wide[plane, :, half] = prod
        parts[plane, :, half] = prod.astype(bf16)
        if half == NC - 1:
            for d in range(1, NX):
                to = (x + d) % NX
                ref = other.at[plane, d - 1]
                remote(parts.at[plane, to], ref, send_sem.at[5], plane_sem.at[0, plane], (row, to)).start()

    def add_up(dz, _):
        _, plane = at(0, dz)
        ref = other.at[plane]
        remote(ref, ref, send_sem.at[5], plane_sem.at[0, plane], (row, x)).wait_recv()
        value = wide[plane, x]
        for d in range(NX - 1):
            value = value + other[plane, d].astype(f32)
        final[plane] = value.astype(bf16)
        spot = plane * (NY * NC) + x * NC + core
        gamma[spot] = final[plane, core]
        remote(final.at[plane, 1 - core], gamma.at[spot], send_sem.at[6], plane_sem.at[1, plane], (mate, x)).start()
        for d in range(1, NX):
            for c in range(NC):
                to = ((z * NY + y) * NC + c, (x + d) % NX)
                remote(final.at[plane, c], gamma.at[spot], send_sem.at[6], plane_sem.at[1, plane], to).start()

    selected = set()

    def select(dz, part):
        _, plane = at(0, dz)
        if part == 0:
            ref = gamma.at[pl.ds(0, NY * NC - 1)]
            remote(ref, ref, send_sem.at[6], plane_sem.at[1, plane], (mate, x)).wait_recv()
        rows = gamma[pl.ds(plane * (NY * NC), NY * NC)].reshape(NY * NC * ROWS, PB)
        lanes = lax.broadcasted_iota(jnp.int32, (1024, 128), 1)
        at_rows = pl.ds(part * 1024, 1024)
        ids = column[at_rows, :] - plane * (NY * NC * ROWS)
        pick = jnp.concatenate(
            [jnp.where(ids == lanes + h * 128, 1.0, 0.0).astype(bf16) for h in range(2)], axis=1
        )
        found = jnp.dot(pick, rows, preferred_element_type=f32)
        if part in selected:
            found = total[at_rows, :] + found
        selected.add(part)
        total[at_rows, :] = found

    def transpose(dz, part):
        _, plane = at(0, dz)
        if part == 0:
            ref = coefs.at[pl.ds(0, NY)]
            remote(ref, ref, send_sem.at[4], plane_sem.at[2, plane], (mate, x)).wait_recv()
        cols = pl.ds(part * 1408, 1408)
        tile = coefs[pl.ds(plane * (NY * NC), NY * NC), :, cols].reshape(128, 1408)
        turned[plane, cols] = jnp.transpose(tile)
        pltpu.make_async_copy(turned.at[plane, cols], ct.at[plane, cols], out_sem.at[0]).start()

    hand_over = pltpu.make_async_copy(rounded, grouped, out_sem.at[1])

    def deliver(_, __):
        rounded[...] = total[...].astype(bf16)
        hand_over.start()

    pass_on(0, 0, 0)
    pass_on(1, 0, 0)
    seen = {}
    for kind, dy, dz in ORDER:
        if kind < 4:
            place = at(dy, dz)
            ref = piece(kind, place)
            remote(ref, ref, send_sem.at[kind], arrival(kind, place), (mate, x)).wait_recv()
            pass_on(kind, dy, dz)
            if kind >= 2:
                seen[dy, dz] = seen.get((dy, dz), 0) + 1
                if seen[dy, dz] == 2:
                    share_coefs(place)
        elif kind == 4:
            pass_on(3, 0, 0)
            pass_on(2, 0, 0)
            share_coefs(at(0, 0))
        else:
            {5: multiply, 6: add_up, 7: select, 8: transpose, 9: prepare, 10: deliver}[kind](dy, dz)

    def drained(ref, sem):
        remote(ref, ref, sem, half_sem.at[1], (mate, x)).wait_send()

    sends = NY * NZ - 1
    drained(blocks.at[pl.ds(0, sends), :, pl.ds(0, KA)], send_sem.at[0])
    drained(blocks.at[pl.ds(0, sends), :, pl.ds(KA, KB - KA)], send_sem.at[1])
    drained(coefs.at[pl.ds(0, sends), :, pl.ds(0, CA)], send_sem.at[2])
    drained(coefs.at[pl.ds(0, sends), :, pl.ds(CA, CP - CA)], send_sem.at[3])
    drained(coefs.at[pl.ds(0, NY * NZ)], send_sem.at[4])
    drained(other, send_sem.at[5])
    drained(gamma.at[pl.ds(0, NZ * (NY * NC - 1))], send_sem.at[6])
    drained(whole, half_sem.at[0])
    hand_over.wait()
    pltpu.make_async_copy(turned, ct, out_sem.at[0]).wait()


def finish(ct, grouped, out, left, right, result, left_sem, right_sem, result_sem):
    tall = CM // CHUNKS
    half = NZ * NY * NC * CR
    get_right = pltpu.make_async_copy(grouped, right, right_sem)
    get_right.start()
    gets = []
    for i in range(CHUNKS):
        rows = pl.ds(i * tall, tall)
        gets.append(pltpu.make_async_copy(ct.at[:, rows], left.at[:, rows], left_sem.at[i]))
        gets[i].start()
    get_right.wait()
    puts = []
    for i in range(CHUNKS):
        rows = pl.ds(i * tall, tall)
        gets[i].wait()
        tile = jnp.concatenate([left[plane, rows] for plane in range(NZ)], axis=1)
        for o in range(2):
            result[o, rows] = jnp.dot(tile, right[pl.ds(o * half, half)], preferred_element_type=jnp.float32)
        puts.append(pltpu.make_async_copy(result.at[:, rows], out.at[:, rows], result_sem.at[i]))
        puts[i].start()
    for put in puts:
        put.wait()


def body(pair_block, resolvent, virt_coef, slot_row):
    dma = pltpu.SemaphoreType.DMA
    bf16, f32 = jnp.bfloat16, jnp.float32
    anywhere = pl.BlockSpec(memory_space=pl.ANY)
    width = NY * NC * CR
    tall = NZ * NY * NC * ROWS
    ct, grouped = pl.pallas_call(
        kernel,
        out_shape=(jax.ShapeDtypeStruct((NZ, CP, width), bf16), jax.ShapeDtypeStruct((tall, PB), bf16)),
        in_specs=[anywhere] * 4,
        out_specs=(anywhere, anywhere),
        scratch_shapes=[
            pltpu.VMEM((NY * NZ, ROWS, KB), bf16),
            pltpu.VMEM((NC, KB, PB), bf16),
            pltpu.VMEM((KB, PB), f32),
            pltpu.VMEM((NY * NZ * NC, CR, CP), bf16),
            pltpu.VMEM((NZ, NY, NC, ROWS, PB), f32),
            pltpu.VMEM((NZ, NY, NC, ROWS, PB), bf16),
            pltpu.VMEM((NZ, NX - 1, NC, ROWS, PB), bf16),
            pltpu.VMEM((NZ, NC, ROWS, PB), bf16),
            pltpu.VMEM((NZ * NY * NC, ROWS, PB), bf16),
            pltpu.VMEM((tall, PB), f32),
            pltpu.VMEM((tall, 128), jnp.int32),
            pltpu.VMEM((CR, CM), bf16),
            pltpu.VMEM((16, 128), jnp.int32),
            pltpu.VMEM((NZ, CP, width), bf16),
            pltpu.VMEM((tall, PB), bf16),
            dma((7,)),
            dma((2,)),
            dma((2, NY * NZ)),
            dma((2, NY * NZ)),
            dma((7,)),
            dma((2,)),
            dma((3, NZ)),
        ],
        compiler_params=pltpu.CompilerParams(
            collective_id=0, has_side_effects=True, vmem_limit_bytes=60 * 1024 * 1024
        ),
    )(pair_block, resolvent, virt_coef, slot_row.reshape(16, 128))
    return pl.pallas_call(
        finish,
        out_shape=jax.ShapeDtypeStruct((2, CM, PB), f32),
        in_specs=[anywhere, anywhere],
        out_specs=anywhere,
        scratch_shapes=[
            pltpu.VMEM((NZ, CP, width), bf16),
            pltpu.VMEM((tall, PB), bf16),
            pltpu.VMEM((2, CM, PB), f32),
            dma((CHUNKS,)),
            dma,
            dma((CHUNKS,)),
        ],
        compiler_params=pltpu.CompilerParams(vmem_limit_bytes=60 * 1024 * 1024),
        cost_estimate=pl.CostEstimate(flops=4 * CM * NZ * width * PB, bytes_accessed=12000000, transcendentals=0),
    )(ct, grouped)


def solution(mesh):
    placed = (P("rows", "panel"), P("panel", "rows"), P("rows", "panel"), P())
    return jax.shard_map(
        body, mesh=mesh, in_specs=placed, out_specs=P(None, "panel", "rows"), check_vma=False
    )
```

time: 114 us -> 94.9 us (0.83)
  Pallas kernels: 106 us -> 94.7 us
  local copies, waits for them, and re-layouts: 7.35 us -> 0 us
    pallas_call x2, Pallas kernels: 106 us -> 94.7 us  [the longest x1 86.8 us: body(): pl.pallas_call(kernel, out_shape=(jax.ShapeDtypeStruct((NZ, CP, width), b...]
    unnamed x10 -> x0, local copies, waits for them, and re-layouts: 7.35 us -> none
where the time goes in v2:
time: 94.9 us; the launch traced here: 94.8 us
  Pallas kernels  94.7 us (100%)
    pallas_call x1, Pallas kernels, body(): pl.pallas_call(kernel, out_shape=(jax.ShapeDtypeStruct((NZ, CP, width), b...  86.8 us
    pallas_call x1, Pallas kernels, body(): pl.pallas_call(finish, out_shape=jax.ShapeDtypeStruct((2, CM, PB), f32),...  7.87 us

profile of v2, /device:TPU:1, one launch (start us, length us, event | category | flops | bytes accessed | tf_op | source)
XLA Modules:
  0.0 94.8 jit_solution(16518875834103751566)
XLA Ops:
  0.0 86.8 %shard_map.46 = (bf16[8,2816,128]{2,1,0:T(8,128)(2,1)}, bf16[2048,256]{1,0:T(8,128)(2,1)}) custom-call(bf16[32,4096]{1,0:T(8,128)(2,1)} %pair.1, f32[4096,256]{1,0:T(8,128)} %res.1, bf16[16,2800]{1,0:T(8,128)(2,1)} %coef.1, s32[16,128]{1,0:T(8,128)} %bitcast.1), custom_call_target="tpu_custom_call" | custom-call | tf_op jit(solution)/shard_map/pallas_call | solution.py:269
  86.8 7.9 %shard_map.47 = f32[2,2800,256]{2,1,0:T(8,128)} custom-call(bf16[8,2816,128]{2,1,0:T(8,128)(2,1)} %get-tuple-element.7.ct, bf16[2048,256]{1,0:T(8,128)(2,1)} %get-tuple-element.8.grouped), custom_call_target="tpu_custom_call" | custom-call | flops 2936012800 | bytes 12000000 | tf_op jit(solution)/shard_map/pallas_call | solution.py:302

commit v3 on v2

--- a/solution.py
+++ b/solution.py
@@ -18,28 +18,28 @@
 ORDER = (
     (9, 0, 0), (9, 1, 0), (9, 2, 0), (9, 3, 0), (9, 4, 0), (9, 5, 0), (0, 1, 0), (0, 3, 0), (0, 0, 1), (0, 0, 7),
     (1, 1, 0), (1, 3, 0), (1, 0, 1), (1, 0, 7), (0, 2, 0), (0, 1, 1), (0, 1, 7), (0, 3, 1), (0, 3, 7), (1, 2, 0),
-    (5, 0, 0), (1, 3, 1), (5, 0, 1), (0, 0, 2), (0, 0, 6), (1, 1, 1), (1, 3, 7), (6, 0, 0), (1, 1, 7), (1, 0, 2),
-    (1, 0, 6), (1, 2, 1), (0, 2, 1), (0, 2, 7), (5, 1, 0), (5, 1, 1), (7, 0, 0), (7, 0, 1), (0, 1, 2), (0, 1, 6),
-    (1, 2, 7), (5, 7, 0), (1, 3, 2), (5, 7, 1), (6, 1, 0), (0, 3, 2), (0, 3, 6), (1, 1, 2), (1, 3, 6), (0, 0, 3),
-    (0, 0, 5), (6, 7, 0), (1, 1, 6), (1, 2, 2), (1, 0, 3), (1, 0, 5), (7, 1, 0), (1, 2, 6), (7, 1, 1), (7, 7, 0),
-    (7, 7, 1), (0, 2, 2), (0, 2, 6), (5, 2, 0), (5, 2, 1), (5, 6, 0), (5, 6, 1), (0, 1, 3), (0, 1, 5), (1, 1, 3),
-    (1, 3, 3), (6, 2, 0), (0, 3, 3), (0, 3, 5), (6, 6, 0), (1, 1, 5), (1, 3, 5), (4, 0, 0), (0, 0, 4), (0, 2, 5),
-    (1, 2, 3), (1, 0, 4), (7, 2, 0), (3, 3, 0), (3, 0, 7), (7, 2, 1), (7, 6, 0), (2, 3, 0), (2, 0, 7), (1, 2, 5),
-    (0, 2, 3), (5, 3, 0), (5, 3, 1), (3, 1, 0), (5, 5, 0), (0, 1, 4), (5, 5, 1), (2, 1, 0), (3, 0, 6), (7, 6, 1),
-    (2, 3, 7), (1, 3, 4), (2, 0, 6), (0, 3, 4), (6, 3, 0), (3, 3, 7), (3, 0, 1), (2, 1, 7), (1, 1, 4), (6, 5, 0),
-    (2, 0, 1), (3, 3, 6), (3, 1, 7), (3, 0, 5), (2, 3, 1), (3, 2, 0), (2, 3, 6), (2, 2, 0), (3, 3, 1), (2, 0, 5),
-    (3, 1, 6), (0, 2, 4), (2, 1, 6), (3, 3, 5), (8, 0, 0), (3, 1, 1), (2, 1, 1), (2, 3, 5), (8, 0, 1), (7, 3, 0),
-    (7, 3, 1), (2, 2, 7), (3, 0, 2), (7, 5, 0), (1, 2, 4), (5, 4, 0), (2, 1, 5), (2, 0, 2), (3, 2, 7), (2, 3, 2),
-    (3, 1, 5), (2, 2, 1), (5, 4, 1), (2, 1, 2), (3, 2, 6), (7, 5, 1), (2, 2, 6), (3, 0, 3), (3, 3, 2), (3, 2, 1),
-    (2, 0, 3), (3, 1, 2), (2, 3, 3), (2, 2, 2), (3, 2, 5), (8, 1, 0), (2, 1, 3), (8, 1, 1), (2, 2, 5), (6, 4, 0),
-    (3, 0, 4), (3, 1, 3), (3, 3, 3), (2, 0, 4), (8, 7, 0), (3, 2, 2), (2, 3, 4), (8, 7, 1), (2, 2, 3), (2, 1, 4),
-    (8, 2, 0), (8, 2, 1), (8, 6, 0), (3, 1, 4), (3, 3, 4), (8, 6, 1), (2, 2, 4), (3, 2, 3), (7, 4, 0), (7, 4, 1),
-    (10, 0, 0), (8, 3, 0), (3, 2, 4), (8, 3, 1), (8, 5, 0), (8, 5, 1), (8, 4, 0), (8, 4, 1),
+    (5, 0, 0), (1, 3, 1), (5, 0, 1), (0, 0, 2), (0, 0, 6), (1, 1, 1), (1, 3, 7), (1, 0, 2), (1, 0, 6), (1, 1, 7),
+    (6, 0, 0), (1, 2, 1), (0, 2, 1), (0, 2, 7), (5, 1, 0), (5, 1, 1), (0, 1, 2), (0, 1, 6), (1, 1, 2), (1, 3, 2),
+    (7, 0, 0), (0, 3, 2), (0, 3, 6), (7, 0, 1), (1, 1, 6), (1, 3, 6), (6, 1, 0), (0, 0, 3), (0, 0, 5), (1, 2, 7),
+    (5, 7, 0), (5, 7, 1), (1, 2, 2), (1, 0, 3), (1, 0, 5), (1, 2, 6), (4, 0, 0), (0, 2, 2), (0, 2, 6), (5, 2, 0),
+    (5, 2, 1), (5, 6, 0), (5, 6, 1), (6, 7, 0), (0, 1, 3), (0, 1, 5), (1, 1, 3), (1, 3, 3), (0, 3, 3), (0, 3, 5),
+    (3, 0, 7), (1, 1, 5), (1, 3, 5), (6, 2, 0), (0, 0, 4), (2, 1, 0), (2, 3, 0), (6, 6, 0), (7, 1, 0), (0, 2, 5),
+    (7, 1, 1), (7, 7, 0), (1, 2, 3), (7, 7, 1), (3, 0, 6), (1, 0, 4), (3, 0, 1), (1, 2, 5), (5, 5, 0), (2, 2, 0),
+    (5, 5, 1), (0, 2, 3), (5, 3, 0), (5, 3, 1), (3, 0, 5), (7, 2, 0), (0, 1, 4), (7, 2, 1), (7, 6, 0), (7, 6, 1),
+    (0, 3, 4), (3, 0, 2), (1, 1, 4), (1, 3, 4), (4, 1, 0), (0, 2, 4), (6, 5, 0), (3, 0, 3), (2, 0, 7), (6, 3, 0),
+    (3, 3, 0), (2, 0, 1), (2, 1, 7), (2, 1, 1), (3, 3, 1), (2, 2, 7), (1, 2, 4), (2, 2, 1), (5, 4, 0), (2, 3, 7),
+    (3, 3, 2), (2, 3, 1), (5, 4, 1), (3, 1, 0), (2, 0, 6), (3, 3, 5), (2, 1, 6), (3, 0, 4), (3, 1, 1), (3, 3, 6),
+    (2, 2, 6), (2, 0, 2), (7, 3, 0), (3, 1, 2), (7, 3, 1), (2, 3, 6), (2, 1, 2), (3, 3, 7), (7, 5, 0), (2, 2, 2),
+    (2, 0, 5), (3, 1, 5), (7, 5, 1), (3, 3, 3), (2, 3, 2), (2, 1, 5), (3, 1, 6), (2, 0, 3), (2, 2, 5), (3, 3, 4),
+    (3, 1, 7), (6, 4, 0), (2, 1, 3), (2, 3, 5), (3, 1, 3), (2, 2, 3), (3, 2, 0), (2, 3, 3), (3, 1, 4), (2, 0, 4),
+    (3, 2, 1), (8, 0, 0), (2, 1, 4), (3, 2, 2), (2, 2, 4), (3, 2, 5), (8, 0, 1), (2, 3, 4), (3, 2, 6), (3, 2, 7),
+    (7, 4, 0), (3, 2, 3), (7, 4, 1), (3, 2, 4), (10, 0, 0), (8, 2, 0), (8, 1, 0), (8, 1, 1), (8, 2, 1), (8, 3, 0),
+    (8, 3, 1), (8, 4, 0), (8, 4, 1), (8, 5, 0), (8, 5, 1), (8, 6, 0), (8, 6, 1), (8, 7, 0), (8, 7, 1),
 )
 
 
 def kernel(pair, res, coef, slots, ct, grouped, blocks, weights, stage, coefs, wide, parts, other, final, gamma, total,
-           column, own_coef, own_slots, turned, rounded, load_sem, out_sem, block_sem, coef_sem, send_sem, half_sem,
+           column, own_coef, own_slots, load_sem, block_sem, coef_sem, send_sem, half_sem,
            plane_sem):
     row, x = lax.axis_index("rows"), lax.axis_index("panel")
     core, y, z = row % NC, (row // NC) % NY, row // (NC * NY)
@@ -89,6 +89,9 @@
     def arrival(kind, place):
         sems = block_sem if kind < 2 else coef_sem
         return sems.at[kind % 2, place[1] * NY + place[0]]
+
+    held = []
+    opened = []
 
     def pass_on(kind, dy, dz):
         place = at(dy, dz)
@@ -108,7 +111,12 @@
             elif dy == 1:
                 along_y = [1]
         for hop in [(d, 0) for d in along_y] + [(0, d) for d in along_z]:
-            remote(ref, ref, send_sem.at[kind], arrival(kind, place), device(*hop)).start()
+            copy = remote(ref, ref, send_sem.at[kind], arrival(kind, place), device(*hop))
+            second = (kind == 2 and dz == 0 and hop[0] == 0) or (kind == 3 and dy == 0 and hop[1] == 0)
+            if second and not opened:
+                held.append((kind, dy + dz, len(held), copy))
+            else:
+                copy.start()
 
     def share_coefs(place):
         ref = coefs.at[(place[1] * NY + place[0]) * NC + core]
@@ -191,14 +199,10 @@
             remote(ref, ref, send_sem.at[4], plane_sem.at[2, plane], (mate, x)).wait_recv()
         cols = pl.ds(part * 1408, 1408)
         tile = coefs[pl.ds(plane * (NY * NC), NY * NC), :, cols].reshape(128, 1408)
-        turned[plane, cols] = jnp.transpose(tile)
-        pltpu.make_async_copy(turned.at[plane, cols], ct.at[plane, cols], out_sem.at[0]).start()
-
-    hand_over = pltpu.make_async_copy(rounded, grouped, out_sem.at[1])
+        ct[plane, cols] = jnp.transpose(tile)
 
     def deliver(_, __):
-        rounded[...] = total[...].astype(bf16)
-        hand_over.start()
+        grouped[...] = total[...].astype(bf16)
 
     pass_on(0, 0, 0)
     pass_on(1, 0, 0)
@@ -213,6 +217,10 @@
                 seen[dy, dz] = seen.get((dy, dz), 0) + 1
                 if seen[dy, dz] == 2:
                     share_coefs(place)
+        elif kind == 4 and dy == 1:
+            for entry in sorted(held, key=lambda entry: entry[:3]):
+                entry[3].start()
+            opened.append(True)
         elif kind == 4:
             pass_on(3, 0, 0)
             pass_on(2, 0, 0)
@@ -232,28 +240,17 @@
     drained(other, send_sem.at[5])
     drained(gamma.at[pl.ds(0, NZ * (NY * NC - 1))], send_sem.at[6])
     drained(whole, half_sem.at[0])
-    hand_over.wait()
-    pltpu.make_async_copy(turned, ct, out_sem.at[0]).wait()
-
-
-def finish(ct, grouped, out, left, right, result, left_sem, right_sem, result_sem):
+
+
+def finish(ct, grouped, out, result, result_sem):
     tall = CM // CHUNKS
     half = NZ * NY * NC * CR
-    get_right = pltpu.make_async_copy(grouped, right, right_sem)
-    get_right.start()
-    gets = []
-    for i in range(CHUNKS):
-        rows = pl.ds(i * tall, tall)
-        gets.append(pltpu.make_async_copy(ct.at[:, rows], left.at[:, rows], left_sem.at[i]))
-        gets[i].start()
-    get_right.wait()
     puts = []
     for i in range(CHUNKS):
         rows = pl.ds(i * tall, tall)
-        gets[i].wait()
-        tile = jnp.concatenate([left[plane, rows] for plane in range(NZ)], axis=1)
+        tile = jnp.concatenate([ct[plane, rows] for plane in range(NZ)], axis=1)
         for o in range(2):
-            result[o, rows] = jnp.dot(tile, right[pl.ds(o * half, half)], preferred_element_type=jnp.float32)
+            result[o, rows] = jnp.dot(tile, grouped[pl.ds(o * half, half)], preferred_element_type=jnp.float32)
         puts.append(pltpu.make_async_copy(result.at[:, rows], out.at[:, rows], result_sem.at[i]))
         puts[i].start()
     for put in puts:
@@ -264,13 +261,15 @@
     dma = pltpu.SemaphoreType.DMA
     bf16, f32 = jnp.bfloat16, jnp.float32
     anywhere = pl.BlockSpec(memory_space=pl.ANY)
+    vmem = pl.BlockSpec(memory_space=pltpu.VMEM)
+    given = (pair_block, resolvent, virt_coef, slot_row.reshape(16, 128))
     width = NY * NC * CR
     tall = NZ * NY * NC * ROWS
     ct, grouped = pl.pallas_call(
         kernel,
         out_shape=(jax.ShapeDtypeStruct((NZ, CP, width), bf16), jax.ShapeDtypeStruct((tall, PB), bf16)),
         in_specs=[anywhere] * 4,
-        out_specs=(anywhere, anywhere),
+        out_specs=(vmem, vmem),
         scratch_shapes=[
             pltpu.VMEM((NY * NZ, ROWS, KB), bf16),
             pltpu.VMEM((NC, KB, PB), bf16),
@@ -285,10 +284,7 @@
             pltpu.VMEM((tall, 128), jnp.int32),
             pltpu.VMEM((CR, CM), bf16),
             pltpu.VMEM((16, 128), jnp.int32),
-            pltpu.VMEM((NZ, CP, width), bf16),
-            pltpu.VMEM((tall, PB), bf16),
             dma((7,)),
-            dma((2,)),
             dma((2, NY * NZ)),
             dma((2, NY * NZ)),
             dma((7,)),
@@ -296,23 +292,19 @@
             dma((3, NZ)),
         ],
         compiler_params=pltpu.CompilerParams(
-            collective_id=0, has_side_effects=True, vmem_limit_bytes=60 * 1024 * 1024
+            collective_id=0, has_side_effects=True, vmem_limit_bytes=40 * 1024 * 1024
         ),
-    )(pair_block, resolvent, virt_coef, slot_row.reshape(16, 128))
+    )(*(pltpu.with_memory_space_constraint(a, pltpu.HBM) for a in given))
     return pl.pallas_call(
         finish,
         out_shape=jax.ShapeDtypeStruct((2, CM, PB), f32),
-        in_specs=[anywhere, anywhere],
+        in_specs=[vmem, vmem],
         out_specs=anywhere,
         scratch_shapes=[
-            pltpu.VMEM((NZ, CP, width), bf16),
-            pltpu.VMEM((tall, PB), bf16),
             pltpu.VMEM((2, CM, PB), f32),
             dma((CHUNKS,)),
-            dma,
-            dma((CHUNKS,)),
         ],
-        compiler_params=pltpu.CompilerParams(vmem_limit_bytes=60 * 1024 * 1024),
+        compiler_params=pltpu.CompilerParams(vmem_limit_bytes=16 * 1024 * 1024),
         cost_estimate=pl.CostEstimate(flops=4 * CM * NZ * width * PB, bytes_accessed=12000000, transcendentals=0),
     )(ct, grouped)
 

time: 94.9 us -> 84.6 us (0.89)
  Pallas kernels: 94.7 us -> 84.4 us
    pallas_call x1, Pallas kernels: 86.8 us -> 80.3 us  [body(): pl.pallas_call(kernel, out_shape=(jax.ShapeDtypeStruct((NZ, CP, width), b...]
    pallas_call x1, Pallas kernels: 7.87 us -> 4.08 us  [body(): pl.pallas_call(finish, out_shape=jax.ShapeDtypeStruct((2, CM, PB), f32),...]
where the time goes in v3:
time: 84.6 us; the launch traced here: 84.5 us
  Pallas kernels  84.4 us (100%)
    pallas_call x1, Pallas kernels, body(): pl.pallas_call(kernel, out_shape=(jax.ShapeDtypeStruct((NZ, CP, width), b...  80.3 us
    pallas_call x1, Pallas kernels, body(): pl.pallas_call(finish, out_shape=jax.ShapeDtypeStruct((2, CM, PB), f32),...  4.08 us

profile of v3, /device:TPU:1, one launch (start us, length us, event | category | flops | bytes accessed | tf_op | source)
XLA Modules:
  0.0 84.5 jit_solution(13596874913094696065)
XLA Ops:
  0.0 80.3 %shard_map.46 = (bf16[8,2816,128]{2,1,0:T(8,128)(2,1)S(1)}, bf16[2048,256]{1,0:T(8,128)(2,1)S(1)}) custom-call(bf16[32,4096]{1,0:T(8,128)(2,1)} %pair.1, f32[4096,256]{1,0:T(8,128)} %res.1, bf16[16,2800]{1,0:T(8,128)(2,1)} %coef.1, s32[16,128]{1,0:T(8,128)} %bitcast.1), custom_call_target="tpu_custom_call" | custom-call | tf_op jit(solution)/shard_map/pallas_call | solution.py:268
  80.3 4.1 %shard_map.47 = f32[2,2800,256]{2,1,0:T(8,128)} custom-call(bf16[8,2816,128]{2,1,0:T(8,128)(2,1)S(1)} %get-tuple-element.7.ct, bf16[2048,256]{1,0:T(8,128)(2,1)S(1)} %get-tuple-element.8.grouped), custom_call_target="tpu_custom_call" | custom-call | flops 2936012800 | bytes 12000000 | tf_op jit(solution)/shard_map/pallas_call | solution.py:298
